TPU v7x, 32 devices: a whole 2x2x4 slice. The times are simulated.
32 devices in a mesh: dp: 4 (over y, x), space: 8 (over z, core).
Axes of the slice: x: 2, y: 2, z: 4, core: 2. Of those that a mesh axis runs over, the one named last changes fastest.
Arguments:
- fields: bfloat16 [4, 100, 32768], P('dp', None, 'space'), may hold values from -6 to 6
- cell_index: int32 [256, 128], P('space'), may hold values from 0 to 6143
- interp_weight: bfloat16 [256, 16, 128], P('space'), may hold values from 0 to 2, as said below
- w_in: bfloat16 [100, 1024], replicated, may hold values from -0.625 to 0.625
- ln_gain: float32 [1024], replicated, may hold values from 0.5 to 1.5
- w_qkv: bfloat16 [1024, 3072], P('dp'), may hold values from -0.1875 to 0.1875
- w_out: bfloat16 [1024, 1024], P('dp'), may hold values from -3 to 3
Outputs:
- latent: bfloat16 [4, 4096, 1024], P('dp', 'space')
- update: bfloat16 [4, 4096, 1024], P('dp', 'space')
Inputs may be any that keep to these rules, and one draw needn't show every extreme that they name: `interp_weight`: in each block the slots from some count on carry zero weight for all its 16 nodes; that count lies between 48 and 128. `cell_index`: indexes a shard's 4096 cells extended by 1024 cells of each neighbouring shard, lower neighbour first.
All inputs are finite; a program needn't handle non-finite values.
Results may differ from a plain program's by a relative error of at most 0.0068.
Values may be sent and summed in bfloat16 or wider, within the bound.
A program may use at most 128 MiB of HBM per device.

v0:
```python
import math

import jax
import jax.numpy as jnp
from jax import lax
from jax.sharding import PartitionSpec as P

HEADS = 16


def padded(array, sides, width):
    for axis, dim in sides:
        size, length = (lax.axis_size(axis), array.shape[dim])
        up = [(i, (i + 1) % size) for i in range(size)]
        down = [(j, i) for i, j in up]
        last = lax.slice_in_dim(array, length - width, length, axis=dim)
        first = lax.slice_in_dim(array, 0, width, axis=dim)
        before = lax.ppermute(last, axis, up)
        after = lax.ppermute(first, axis, down)
        array = jnp.concatenate([before, array, after], axis=dim)
    return array


def unit_heads(projected):
    head_size = projected.shape[1] // HEADS
    head_rows = projected.reshape(projected.shape[0], HEADS, head_size)
    scale_rows = jnp.sqrt(jnp.mean(head_rows * head_rows, axis=-1, keepdims=True) + 1e-06)
    return (head_rows / scale_rows).astype(jnp.bfloat16).reshape(projected.shape)


def shards(fields, cell_index, interp_weight, w_in, ln_gain, w_qkv, w_out):
    width = w_qkv.shape[1] // 3
    full_qkv, full_out = (
        lax.all_gather(w_qkv, "dp", axis=0, tiled=True),
        lax.all_gather(w_out, "dp", axis=0, tiled=True),
    )
    grid_field = fields[0]
    cell_count = grid_field.shape[1]
    cell_reach = cell_count // 4
    extended = padded(grid_field, (("space", 1),), cell_reach)
    picked = jnp.take(extended, cell_index, axis=1)
    encoded = jnp.einsum("cbs,bns->bnc", picked, interp_weight, preferred_element_type=jnp.float32)
    node_count = encoded.shape[0] * encoded.shape[1]
    encoded = encoded.reshape(node_count, encoded.shape[2]).astype(jnp.bfloat16)
    embedded = jnp.dot(encoded, w_in, preferred_element_type=jnp.float32)
    average = jnp.mean(embedded, axis=1, keepdims=True)
    centered = embedded - average
    spread = jnp.mean(centered * centered, axis=1, keepdims=True)
    normed = (centered / jnp.sqrt(spread + 1e-05) * ln_gain).astype(jnp.bfloat16)
    margin = node_count // 2
    projected = jnp.dot(normed, full_qkv, preferred_element_type=jnp.float32)
    queries = unit_heads(projected[:, :width])
    own_pairs = jnp.concatenate(
        [
            unit_heads(projected[:, width : 2 * width]),
            projected[:, 2 * width :].astype(jnp.bfloat16),
        ],
        axis=1,
    )
    window = padded(own_pairs, (("space", 0),), margin)
    head_size = width // HEADS
    group_width = 2 * head_size

    def attend(group_index):
        offset = group_index * group_width
        query_group = lax.dynamic_slice_in_dim(queries, offset, group_width, 1).reshape(
            node_count, 2, head_size
        )
        key_group = lax.dynamic_slice_in_dim(window, offset, group_width, 1).reshape(
            window.shape[0], 2, head_size
        )
        value_group = lax.dynamic_slice_in_dim(window, width + offset, group_width, 1).reshape(
            window.shape[0], 2, head_size
        )
        scores = jnp.einsum(
            "qhd,khd->hqk", query_group, key_group, preferred_element_type=jnp.float32
        ) / math.sqrt(head_size)
        weights = jnp.exp(scores)
        probs = (weights / jnp.sum(weights, axis=2, keepdims=True)).astype(jnp.bfloat16)
        mixed_rows = jnp.einsum(
            "hqk,khd->qhd", probs, value_group, preferred_element_type=jnp.float32
        )
        return mixed_rows.astype(jnp.bfloat16).reshape(node_count, group_width)

    grouped = lax.map(attend, jnp.arange(HEADS // 2, dtype=jnp.int32))
    attended = grouped.transpose(1, 0, 2).reshape(node_count, width)
    update = jnp.dot(attended, full_out, preferred_element_type=jnp.float32)
    return (embedded.astype(jnp.bfloat16)[None], update.astype(jnp.bfloat16)[None])


def solution(mesh):
    placed = (
        P("dp", None, "space"),
        P("space", None),
        P("space", None, None),
        P(),
        P(),
        P("dp", None),
        P("dp", None),
    )
    return jax.shard_map(
        shards,
        mesh=mesh,
        in_specs=placed,
        out_specs=(P("dp", "space", None), P("dp", "space", None)),
        check_vma=False,
    )
```

profile of v0, /device:TPU:1, one launch (start us, length us, event | category | flops | bytes accessed | tf_op | source)
XLA Modules:
  0.0 190.7 jit_solution(8053254927980456501)
XLA Ops:
  7.2 0.7 all-gather.3.cloned.1.call-update
  8.0 0.4 copy-done.3
  8.4 0.7 copy.13
  9.1 2.7 %collective-permute-start = (bf16[100,1024]{0,1:T(8,128)(2,1)S(1)}, bf16[100,1024]{0,1:T(8,128)(2,1)S(1)}, u32[]{:S(2)}, u32[]{:S(2)}) collective-permute-start(bf16[100,1024]{0,1:T(8,128)(2,1)S(1)} %get-tuple-element.100), channel_id=1, source_target_pairs={{0,1},{1,2},{2,3},{3,4},{4,5},{5,6},{6,7},{7,0},{8,9},{9,10},{10,1... | collective-permute-start | bytes 614408 | tf_op jit(solution)/shard_map/ppermute | solution.py:18
  11.9 4.0 %collective-permute-done = bf16[100,1024]{0,1:T(8,128)(2,1)S(1)} collective-permute-done((bf16[100,1024]{0,1:T(8,128)(2,1)S(1)}, bf16[100,1024]{0,1:T(8,128)(2,1)S(1)}, u32[]{:S(2)}, u32[]{:S(2)}) %collective-permute-start) | collective-permute-done | bytes 204832 | tf_op jit(solution)/shard_map/ppermute | solution.py:18
  15.8 4.0 %collective-permute-done.1 = bf16[100,1024]{0,1:T(8,128)(2,1)S(1)} collective-permute-done((bf16[100,1024]{0,1:T(8,128)(2,1)S(1)}, bf16[100,1024]{0,1:T(8,128)(2,1)S(1)}, u32[]{:S(2)}, u32[]{:S(2)}) %collective-permute-start.1) | collective-permute-done | bytes 204832 | tf_op jit(solution)/shard_map/ppermute | solution.py:19
  19.9 0.3 pad_maximum_fusion.1
  20.2 12.1 %gather_fusion = bf16[4096,100]{1,0:T(8,128)(2,1)S(1)} fusion(bf16[100,6144]{0,1:T(8,128)(2,1)S(1)} %pad_maximum_fusion.1, s32[4096]{0:T(1024)S(1)} %bitcast_clamp_fusion), kind=kCustom, calls=%fused_computation | custom fusion | bytes 1654784 | tf_op jit(solution)/shard_map/jit(_take)/gather | solution.py:41
  32.3 0.7 copy.14
  33.0 0.5 convolution_convert_fusion.1
  33.6 0.5 fusion.16
  34.1 1.4 multiply_reduce_fusion
  35.5 46.3 %all-gather.3.cloned.1.call-done = bf16[1024,3072]{1,0:T(8,128)(2,1)} async-done(((bf16[256,3072]{1,0:T(8,128)(2,1)}), bf16[1024,3072]{1,0:T(8,128)(2,1)}) %all-gather.3.cloned.1.call-update) | async-done | bytes 6291472 | tf_op jit(solution)/shard_map/all_gather | solution.py:34
  81.8 5.8 %fusion.5 = f32[512,3072]{1,0:T(8,128)S(1)} fusion(bf16[1024,3072]{1,0:T(8,128)(2,1)} %all-gather.3.cloned.1.call-done, f32[512,1024]{1,0:T(8,128)S(1)} %get-tuple-element.103, f32[1024]{0:T(1024)S(1)} %copy-done.6, f32[512]{0:T(512)S(1)} %add_sqrt_fusion.2, f32[512]{0:T(512)S(1)} %broadcast_multiply_fusion), kind=kOutput, calls=%fused_computation.27 | convolution fusion | flops 3223322624 | bytes 14688256 | tf_op jit(solution)/shard_map/dot_general | solution.py:51
  87.6 3.2 %slice_multiply_fusion = (f32[512,1024]{1,0:T(8,128)}, f32[512,1024]{1,0:T(8,128)}) fusion(f32[512,3072]{1,0:T(8,128)S(1)} %fusion.5), kind=kLoop, calls=%fused_computation.21 | loop fusion | flops 1048576 | bytes 8388608 | tf_op jit(solution)/shard_map/mul | solution.py:27
  90.8 0.7 copy-done.1
  91.8 1.9 %copy.15 = f32[512,1024]{0,1:T(8,128)S(1)} copy(f32[512,1024]{1,0:T(8,128)} %get-tuple-element.95) | data formatting | bytes 4194304 | tf_op jit(solution)/shard_map/mul | solution.py:27
  93.7 0.3 bitcast_reduce_fusion.1
  94.0 0.3 div.64
  94.3 1.9 copy.16
  96.1 1.9 %copy.17 = f32[512,1024]{0,1:T(8,128)S(1)} copy(f32[512,1024]{1,0:T(8,128)} %get-tuple-element.94) | data formatting | bytes 4194304 | tf_op jit(solution)/shard_map/mul | solution.py:27
  98.0 0.3 bitcast_reduce_fusion
  98.6 1.9 copy.18
  100.5 4.3 %divide_convert_fusion.4 = (bf16[512,1024]{1,0:T(8,128)(2,1)S(1)}, bf16[512,1024]{1,0:T(8,128)(2,1)S(1)}) fusion(f32[512,1024]{1,0:T(8,128)} %copy.18, f32[512,3072]{1,0:T(8,128)} %copy-done.1, f32[512,1024]{1,0:T(8,128)} %copy.16), kind=kLoop, calls=%fused_computation.17 | loop fusion | flops 2097152 | bytes 10485760 | tf_op jit(solution)/shard_map/convert_element_type | solution.py:28
  104.8 1.5 fusion.6
  106.3 1.9 %collective-permute-start.2 = (bf16[256,2048]{1,0:T(8,128)(2,1)}, bf16[256,2048]{1,0:T(8,128)(2,1)}, u32[]{:S(2)}, u32[]{:S(2)}) collective-permute-start(bf16[256,2048]{1,0:T(8,128)(2,1)} %get-tuple-element.96), channel_id=1, source_target_pairs={{0,1},{1,2},{2,3},{3,4},{4,5},{5,6},{6,7},{7,0},{8,9},{9,10},{10,1... | collective-permute-start | bytes 3145736 | tf_op jit(solution)/shard_map/ppermute | solution.py:18
  108.3 20.6 %collective-permute-done.2 = bf16[256,2048]{1,0:T(8,128)(2,1)} collective-permute-done((bf16[256,2048]{1,0:T(8,128)(2,1)}, bf16[256,2048]{1,0:T(8,128)(2,1)}, u32[]{:S(2)}, u32[]{:S(2)}) %collective-permute-start.2) | collective-permute-done | bytes 1048608 | tf_op jit(solution)/shard_map/ppermute | solution.py:18
  128.9 5.4 %collective-permute-done.3 = bf16[256,2048]{1,0:T(8,128)(2,1)} collective-permute-done((bf16[256,2048]{1,0:T(8,128)(2,1)}, bf16[256,2048]{1,0:T(8,128)(2,1)}, u32[]{:S(2)}, u32[]{:S(2)}) %collective-permute-start.3) | collective-permute-done | bytes 1048608 | tf_op jit(solution)/shard_map/ppermute | solution.py:19
  134.3 4.1 %pad_maximum_fusion = bf16[1024,2048]{1,0:T(8,128)(2,1)} fusion(bf16[256,2048]{1,0:T(8,128)(2,1)} %collective-permute-done.3, bf16[512,1024]{1,0:T(8,128)(2,1)S(1)} %slice.49, bf16[512,1024]{1,0:T(8,128)(2,1)S(1)} %get-tuple-element.93, bf16[256,2048]{1,0:T(8,128)(2,1)} %collective-permute-done.2), kind=kLoop, calls=%fused_computation.11 | loop fusion | flops 16777216 | bytes 8388608 | tf_op jit(solution)/shard_map/concatenate | solution.py:20
  138.4 6.5 %copy.19 = bf16[1024,2048]{0,1:T(8,128)(2,1)} copy(bf16[1024,2048]{1,0:T(8,128)(2,1)} %pad_maximum_fusion) | data formatting | bytes 8388608 | tf_op jit(solution)/shard_map/while | solution.py:85
  144.9 35.0 %while.12 = (s32[]{:T(128)}, bf16[8,512,128]{1,2,0:T(8,128)(2,1)S(1)}, s32[8]{0:T(128)S(1)}, bf16[1024,2048]{0,1:T(8,128)(2,1)}, bf16[512,1024]{1,0:T(8,128)(2,1...) while((s32[]{:T(128)}, ...), condition=%wide.region_6.7_spmd, body=%wide.region_4.6_spmd.sunk | while | flops 273742848 | bytes 11018482 | solution.py:85
  144.9 0.6 dynamic_slice.33
  146.2 1.1 constant_dynamic-slice_fusion.5
  147.4 0.9 fusion.34
  148.3 0.9 fusion.35
  149.3 0.6 dynamic_slice.33
  150.6 1.1 constant_dynamic-slice_fusion.5
  151.8 0.9 fusion.34
  152.7 0.9 fusion.35
  153.7 0.6 dynamic_slice.33
  155.0 1.1 constant_dynamic-slice_fusion.5
  156.2 0.9 fusion.34
  157.1 0.9 fusion.35
  158.1 0.6 dynamic_slice.33
  159.3 1.1 constant_dynamic-slice_fusion.5
  160.6 0.9 fusion.34
  161.5 0.9 fusion.35
  162.5 0.6 dynamic_slice.33
  163.7 1.1 constant_dynamic-slice_fusion.5
  165.0 0.9 fusion.34
  165.9 0.9 fusion.35
  166.8 0.6 dynamic_slice.33
  168.1 1.1 constant_dynamic-slice_fusion.5
  169.3 0.9 fusion.34
  170.2 0.9 fusion.35
  171.2 0.6 dynamic_slice.33
  172.5 1.1 constant_dynamic-slice_fusion.5
  173.7 0.9 fusion.34
  174.6 0.9 fusion.35
  175.6 0.6 dynamic_slice.33
  176.8 1.1 constant_dynamic-slice_fusion.5
  178.1 0.9 fusion.34
  179.0 0.9 fusion.35
  180.0 3.8 %fusion.4 = bf16[1,512,1024]{2,1,0:T(8,128)(2,1)} fusion(bf16[512,1024]{0,1:T(8,128)(2,1)S(1)} %bitcast.64, bf16[1024,1024]{1,0:T(8,128)(2,1)} %all-gather.5.cloned.1.call-done), kind=kOutput, calls=%fused_computation.25 | convolution fusion | flops 1074266112 | bytes 4194304 | tf_op jit(solution)/shard_map/dot_general | solution.py:87
  (53 shorter events, 2.0 us)
Async XLA Ops:
  7.2 26.4 %copy-start = (bf16[100,1024]{1,0:T(8,128)(2,1)S(1)}, bf16[100,1024]{1,0:T(8,128)(2,1)}, u32[]{:S(2)}) copy-start(bf16[100,1024]{1,0:T(8,128)(2,1)} %param.12) | copy-start | bytes 614404
  7.2 1.2 copy-start.3
  7.2 74.6 %all-gather.3.cloned.1.call-start = ((), (), s32[]{:S(2)}) async-start(), calls=%async_computation | async-start | bytes 7864320 | tf_op jit(solution)/shard_map/all_gather | solution.py:34
  7.2 4.6 %copy-start.4 = (s32[32,128]{1,0:T(8,128)S(1)}, s32[32,128]{1,0:T(8,128)}, u32[]{:S(2)}) copy-start(s32[32,128]{1,0:T(8,128)} %param.10) | copy-start | bytes 49156
  7.9 172.1 %all-gather.5.cloned.1.call-start = ((), (), s32[]{:S(2)}) async-start(), calls=%async_computation.1 | async-start | bytes 2621440 | tf_op jit(solution)/shard_map/all_gather | solution.py:35
  9.1 6.7 %collective-permute-start = (bf16[100,1024]{0,1:T(8,128)(2,1)S(1)}, bf16[100,1024]{0,1:T(8,128)(2,1)S(1)}, u32[]{:S(2)}, u32[]{:S(2)}) collective-permute-start(bf16[100,1024]{0,1:T(8,128)(2,1)S(1)} %get-tuple-element.100), channel_id=1, source_target_pairs={{0,1},{1,2},{2,3},{3,4},{4,5},{5,6},{6,7},{7,0},{8,9},{9,10},{10,1... | collective-permute-start | bytes 614408 | tf_op jit(solution)/shard_map/ppermute | solution.py:18
  11.8 8.0 %collective-permute-start.1 = (bf16[100,1024]{0,1:T(8,128)(2,1)S(1)}, bf16[100,1024]{0,1:T(8,128)(2,1)S(1)}, u32[]{:S(2)}, u32[]{:S(2)}) collective-permute-start(bf16[100,1024]{0,1:T(8,128)(2,1)S(1)} %get-tuple-element.101), channel_id=1, source_target_pairs={{1,0},{2,1},{3,2},{4,3},{5,4},{6,5},{7,6},{0,7},{9,8},{10,9},{11,1... | collective-permute-start | bytes 614408 | tf_op jit(solution)/shard_map/ppermute | solution.py:19
  20.2 12.8 %copy-start.5 = (bf16[32,16,128]{2,1,0:T(8,128)(2,1)S(1)}, bf16[32,16,128]{2,1,0:T(8,128)(2,1)}, u32[]{:S(2)}) copy-start(bf16[32,16,128]{2,1,0:T(8,128)(2,1)} %param.11) | copy-start | bytes 393220
  34.1 47.7 %copy-start.6 = (f32[1024]{0:T(1024)S(1)}, f32[1024]{0:T(1024)}, u32[]{:S(2)}) copy-start(f32[1024]{0:T(1024)} %param.13) | copy-start | bytes 12292
  87.6 4.0 %copy-start.1 = (f32[512,3072]{1,0:T(8,128)}, f32[512,3072]{1,0:T(8,128)S(1)}, u32[]{:S(2)}) copy-start(f32[512,3072]{1,0:T(8,128)S(1)} %fusion.5) | copy-start | bytes 18874372
  106.3 22.6 %collective-permute-start.2 = (bf16[256,2048]{1,0:T(8,128)(2,1)}, bf16[256,2048]{1,0:T(8,128)(2,1)}, u32[]{:S(2)}, u32[]{:S(2)}) collective-permute-start(bf16[256,2048]{1,0:T(8,128)(2,1)} %get-tuple-element.96), channel_id=1, source_target_pairs={{0,1},{1,2},{2,3},{3,4},{4,5},{5,6},{6,7},{7,0},{8,9},{9,10},{10,1... | collective-permute-start | bytes 3145736 | tf_op jit(solution)/shard_map/ppermute | solution.py:18
  108.3 26.1 %collective-permute-start.3 = (bf16[256,2048]{1,0:T(8,128)(2,1)}, bf16[256,2048]{1,0:T(8,128)(2,1)}, u32[]{:S(2)}, u32[]{:S(2)}) collective-permute-start(bf16[256,2048]{1,0:T(8,128)(2,1)} %get-tuple-element.97), channel_id=1, source_target_pairs={{1,0},{2,1},{3,2},{4,3},{5,4},{6,5},{7,6},{0,7},{9,8},{10,9},{11,1... | collective-permute-start | bytes 3145736 | tf_op jit(solution)/shard_map/ppermute | solution.py:19
  138.4 6.5 %copy-start.2 = (bf16[8,512,128]{1,2,0:T(8,128)(2,1)S(1)}, bf16[8,512,128]{1,2,0:T(8,128)(2,1)}, u32[]{:S(2)}) copy-start(bf16[8,512,128]{1,2,0:T(8,128)(2,1)} %custom-call.2) | copy-start | bytes 3145732
Sparse Core Ops, SparseCore 0:
  9.8 71.9 all-gather.2
  108.4 34.9 all-gather.4
where the time goes:
time: 191 us
  waiting for transfers between devices  81 us (42%)
  local copies, waits for them, and re-layouts  44 us (23%)
  matrix products  25.3 us (13%)
  other arithmetic  15.5 us (8%)
  between operations  14.3 us (7%)
  loops' own time  5.78 us (3%)
  starting transfers between devices  4.75 us (2%)
    all_gather x1, waiting for transfers between devices, shards(): lax.all_gather(w_qkv, 'dp', axis=0, tiled=True)  46.3 us
    ppermute x2, waiting for transfers between devices, padded(): before = lax.ppermute(last, axis, up)  24.6 us
    gather x2, local copies, waits for them, and re-layouts, shards(): picked = jnp.take(extended, cell_index, axis=1)  12.8 us
    ppermute x2, waiting for transfers between devices, padded(): after = lax.ppermute(first, axis, down)  9.43 us
    dynamic_slice x8, local copies, waits for them, and re-layouts, attend(): lax.dynamic_slice_in_dim(window, offset, group_width, 1)  8.56 us
    dot_general x8, matrix products, attend(): jnp.einsum('hqk,khd->qhd', probs, value_group, preferred_element_type=jnp...  7.36 us
    dot_general x8, matrix products, attend(): jnp.einsum('qhd,khd->hqk', query_group, key_group, preferred_element_type...  7.22 us
    while x1, local copies, waits for them, and re-layouts, shards(): grouped = lax.map(attend, jnp.arange(HEADS // 2, dtype=jnp.int32))  6.49 us
  transfers between devices with their start and end apart: 6, of which 5 were waited for; matrix products, arithmetic and copies ran while one was open for 29% of the time, Pallas kernels for 0%

commit v1 on v0

v1 whole, which is shorter than its diff:
```python
import functools

import jax
import jax.numpy as jnp
from jax import lax
from jax.experimental import pallas as pl
from jax.experimental.pallas import tpu as pltpu
from jax.sharding import PartitionSpec as P

HEADS = 16
GROUP_HEADS = 4
F32, BF16 = jnp.float32, jnp.bfloat16
MESH = pl.DeviceIdType.MESH


def kernel(
    n, space, index_ref, field_ref, weight_ref, w_in_ref, gain_ref, w_qkv_ref, w_out_ref,
    latent_ref, update_ref,
    low_ref, high_ref, cells_ref, picked_ref, enc_ref, w_in_full, normed_ref, qkv_ref, out_ref,
    q_ref, k_ref, v_ref, att_ref,
    local_sem, field_send, field_recv, enc_send, enc_recv,
    a_send, a_recv, f_send, f_recv, p_send, p_recv,
):
    d, s = lax.axis_index("dp"), lax.axis_index("space")
    up, down = lax.rem(s + 1, space), lax.rem(s + space - 1, space)
    core = lax.rem(s, 2)
    partner = s + 1 - 2 * core
    channels, cell_count = field_ref.shape
    reach = low_ref.shape[1]
    rows = w_qkv_ref.shape[0]
    half = rows // 2
    quarter = half // 2
    width = w_out_ref.shape[1]
    groups, _, gw3 = qkv_ref.shape
    gw = gw3 // 3
    head_size = gw // GROUP_HEADS
    nodes = latent_ref.shape[0]
    margin = nodes // 2
    window = nodes + 2 * margin
    blocks, per_block, slots = weight_ref.shape
    if n == 4:
        peers = [d + 1 - 2 * lax.rem(d, 2), lax.rem(d + 2, 4), 3 - d]
    else:
        peers = [lax.rem(d + i, n) for i in range(1, n)]

    local = []
    for g in range(groups):
        for t in range(3):
            local.append(pltpu.make_async_copy(
                w_qkv_ref.at[:, pl.ds(t * width + g * gw, gw)],
                qkv_ref.at[g, pl.ds(pl.multiple_of(d * rows, rows), rows), pl.ds(t * gw, gw)],
                local_sem.at[len(local)]))
    local.append(pltpu.make_async_copy(
        w_out_ref, out_ref.at[pl.ds(pl.multiple_of(d * rows, rows), rows), :],
        local_sem.at[len(local)]))
    for copy in local:
        copy.start()

    barrier = pltpu.get_barrier_semaphore()
    for peer in peers:
        pl.semaphore_signal(barrier, inc=1, device_id=(peer, s), device_id_type=MESH)
    for peer in (up, down):
        pl.semaphore_signal(barrier, inc=1, device_id=(d, peer), device_id_type=MESH)
    pl.semaphore_wait(barrier, len(peers) + 2)

    def remote(src, dst, send, recv, device):
        return pltpu.make_async_remote_copy(
            src_ref=src, dst_ref=dst, send_sem=send, recv_sem=recv,
            device_id=device, device_id_type=MESH)

    field_up = remote(field_ref.at[:, pl.ds(cell_count - reach, reach)], low_ref,
                      field_send.at[0], field_recv.at[0], (d, up))
    field_down = remote(field_ref.at[:, pl.ds(0, reach)], high_ref,
                        field_send.at[1], field_recv.at[1], (d, down))
    field_up.start()
    field_down.start()

    def piece(c, slot, lo, size):
        span = pl.ds(pl.multiple_of(slot * rows + lo, size), size)
        return out_ref.at[span, :] if c == groups else qkv_ref.at[c, span, :]

    def own_copy(c, i):
        ref = piece(c, d, core * half, half)
        return remote(ref, ref, a_send.at[c, i], a_recv.at[c, i], (peers[i], s))

    def own_recv(c, i):
        source = peers[i] if n == 4 else peers[n - 2 - i]
        ref = piece(c, source, core * half, half)
        return remote(ref, ref, a_send.at[c, i], a_recv.at[c, i], (peers[i], s)), source

    def swap(c, i, slot, side):
        ref = piece(c, slot, side * half, half)
        return remote(ref, ref, p_send.at[c, i], p_recv.at[c, i], (d, partner))

    direct = 2 if n == 4 else n - 1

    def begin(c):
        mine = local[3 * c:3 * c + 3] if c < groups else local[-1:]
        for copy in mine:
            copy.wait()
        for i in range(direct):
            own_copy(c, i).start()

    def onward(c, i, slot):
        ref = piece(c, slot, core * half + i * quarter, quarter)
        return remote(ref, ref, f_send.at[c, i], f_recv.at[c, i], (peers[1 - i], s))

    def forward(c):
        for i in range(direct):
            copy, source = own_recv(c, i)
            copy.wait_recv()
            if n == 4:
                onward(c, i, source).start()
            swap(c, i, source, core).start()

    def finish(c):
        if n == 4:
            for i in range(2):
                onward(c, i, peers[2]).wait_recv()
            swap(c, 2, peers[2], core).start()
        for i in range(n - 1):
            source = peers[i] if n == 4 else peers[n - 2 - i]
            swap(c, i, source, 1 - core).wait_recv()

    def drain(c):
        for i in range(direct):
            own_copy(c, i).wait_send()
        if n == 4:
            for i in range(2):
                onward(c, i, peers[i]).wait_send()
        for i in range(n - 1):
            source = peers[i] if n == 4 else peers[n - 2 - i]
            swap(c, i, source, core).wait_send()

    begin(0)
    begin(1)

    unit = (lax.broadcasted_iota(jnp.int32, (channels, 128), 0)
            == lax.broadcasted_iota(jnp.int32, (channels, 128), 1)).astype(BF16)

    def turn(source, start, target):
        cells_ref[pl.ds(target, 512), :] = lax.dot_general(
            source[:, pl.ds(start, 512)], unit, (((0,), (0,)), ((), ())),
            preferred_element_type=F32)

    @pl.loop(0, cell_count // 512)
    def _(i):
        turn(field_ref, pl.multiple_of(i * 512, 512), pl.multiple_of(reach + i * 512, 512))

    pad = w_in_full.shape[0]
    w_in_full[pl.ds(pad - 32, 32), :] = jnp.zeros((32, width), BF16)
    w_in_full[pl.ds(0, channels), :] = w_in_ref[...]

    field_up.wait_recv()
    field_down.wait_recv()

    @pl.loop(0, reach // 512)
    def _(i):
        turn(low_ref, pl.multiple_of(i * 512, 512), pl.multiple_of(i * 512, 512))
        turn(high_ref, pl.multiple_of(i * 512, 512),
             pl.multiple_of(reach + cell_count + i * 512, 512))

    def gather(first, last):
        @pl.loop(first, last)
        def _(b):
            base = pl.multiple_of(b * slots, slots)
            for j in range(slots):
                picked_ref[pl.ds(base + j, 1), :] = cells_ref[pl.ds(index_ref[b, j], 1), :]

    gather(0, blocks // 2)
    forward(0)
    begin(2)
    gather(blocks // 2, blocks)

    per_step = 8

    @pl.loop(0, blocks // per_step)
    def _(i):
        for j in range(per_step):
            b = i * per_step + j
            rows_b = picked_ref[pl.ds(pl.multiple_of(b * slots, slots), slots), :].astype(BF16)
            enc_ref[pl.ds(pl.multiple_of(margin + b * per_block, per_block), per_block), :] = jnp.dot(
                weight_ref[b], rows_b, preferred_element_type=F32).astype(BF16)

    enc_up = remote(enc_ref.at[pl.ds(nodes, margin), :], enc_ref.at[pl.ds(0, margin), :],
                    enc_send.at[0], enc_recv.at[0], (d, up))
    enc_down = remote(enc_ref.at[pl.ds(margin, margin), :],
                      enc_ref.at[pl.ds(margin + nodes, margin), :],
                      enc_send.at[1], enc_recv.at[1], (d, down))
    enc_up.start()
    enc_down.start()
    forward(1)
    begin(3)

    def embed(start, own):
        embedded = jnp.dot(enc_ref[pl.ds(start, 128), :], w_in_full[...], preferred_element_type=F32)
        if own:
            latent_ref[pl.ds(start - margin, 128), :] = embedded.astype(BF16)
        average = jnp.mean(embedded, axis=1, keepdims=True)
        centered = embedded - average
        spread = jnp.mean(centered * centered, axis=1, keepdims=True)
        normed_ref[pl.ds(start, 128), :] = (
            centered * lax.rsqrt(spread + 1e-05) * gain_ref[...]).astype(BF16)

    @pl.loop(0, nodes // 128)
    def _(i):
        embed(pl.multiple_of(margin + i * 128, 128), True)

    enc_up.wait_recv()
    enc_down.wait_recv()

    @pl.loop(0, margin // 128)
    def _(i):
        embed(pl.multiple_of(i * 128, 128), False)
        embed(pl.multiple_of(margin + nodes + i * 128, 128), False)

    forward(2)
    begin(4)

    same_head = (lax.broadcasted_iota(jnp.int32, (gw, gw), 0) // head_size
                 == lax.broadcasted_iota(jnp.int32, (gw, gw), 1) // head_size).astype(BF16)
    contract_last = (((1,), (1,)), ((), ()))

    def unit_heads(block, scale):
        squares = block * block
        high = squares.astype(BF16)
        rest = (squares - high.astype(F32)).astype(BF16)
        total = (jnp.dot(high, same_head, preferred_element_type=F32)
                 + jnp.dot(rest, same_head, preferred_element_type=F32))
        return (block * lax.rsqrt(total * (1.0 / head_size) + 1e-06)).astype(BF16) * scale

    def compute(g):
        @pl.loop(0, window // 256)
        def _(i):
            span = pl.ds(pl.multiple_of(i * 256, 256), 256)
            part = jnp.dot(normed_ref[span, :], qkv_ref[g, :, pl.ds(gw, 2 * gw)],
                           preferred_element_type=F32)
            k_ref[span, :] = unit_heads(part[:, :gw], jnp.asarray(1.0, BF16))
            v_ref[span, :] = part[:, gw:].astype(BF16)

        scale = jnp.asarray(head_size ** -0.5, BF16)

        @pl.loop(0, nodes // 256)
        def _(i):
            part = jnp.dot(normed_ref[pl.ds(pl.multiple_of(margin + i * 256, 256), 256), :],
                           qkv_ref[g, :, pl.ds(0, gw)], preferred_element_type=F32)
            q_ref[pl.ds(pl.multiple_of(i * 256, 256), 256), :] = unit_heads(part, scale)

        @pl.loop(0, nodes // 128)
        def _(i):
            span = pl.ds(pl.multiple_of(i * 128, 128), 128)
            queries = q_ref[span, :]
            head_of = lax.broadcasted_iota(jnp.int32, (128, gw), 1) // head_size
            mixed = jnp.zeros((128, gw), F32)
            for h in range(GROUP_HEADS):
                mine = head_of == h
                scores = lax.dot_general(jnp.where(mine, queries, jnp.zeros_like(queries)),
                                         k_ref[...], contract_last, preferred_element_type=F32)
                weights = jnp.exp(scores)
                total = jnp.sum(weights, axis=1, keepdims=True)
                out = jnp.dot(weights.astype(BF16), v_ref[...], preferred_element_type=F32)
                mixed = jnp.where(mine, out * (1.0 / total), mixed)
            att_ref[g, span, :] = mixed.astype(BF16)

    @pl.loop(0, groups)
    def _(g):
        for c in range(groups):
            @pl.when(g == c)
            def _():
                finish(c)
                if c + 3 <= groups:
                    if c + 3 > 2:
                        forward(c + 3)
        compute(g)

    finish(groups)

    @pl.loop(0, nodes // 128)
    def _(i):
        span = pl.ds(pl.multiple_of(i * 128, 128), 128)
        total = jnp.zeros((128, width), F32)
        for g in range(groups):
            total += jnp.dot(att_ref[g, span, :], out_ref[pl.ds(g * gw, gw), :],
                             preferred_element_type=F32)
        update_ref[span, :] = total.astype(BF16)

    for copy in (field_up, field_down, enc_up, enc_down):
        copy.wait_send()
    for c in range(groups + 1):
        drain(c)


def shards(n, space, fields, cell_index, interp_weight, w_in, ln_gain, w_qkv, w_out):
    width = w_out.shape[1]
    blocks, per_block, _ = interp_weight.shape
    nodes = blocks * per_block
    channels, cells = fields.shape[1:]
    reach = cells // 4
    gw = width // HEADS * GROUP_HEADS
    groups = width // gw
    vmem = pl.BlockSpec(memory_space=pltpu.VMEM)
    hbm = pl.BlockSpec(memory_space=pl.ANY)
    dma = pltpu.SemaphoreType.DMA
    latent, update = pl.pallas_call(
        functools.partial(kernel, n, space),
        out_shape=[jax.ShapeDtypeStruct((nodes, width), BF16)] * 2,
        in_specs=[pl.BlockSpec(memory_space=pltpu.SMEM), vmem, vmem, vmem, vmem, hbm, hbm],
        out_specs=[vmem, vmem],
        scratch_shapes=[
            pltpu.VMEM((channels, reach), BF16),
            pltpu.VMEM((channels, reach), BF16),
            pltpu.VMEM((cells + 2 * reach, 128), F32),
            pltpu.VMEM((blocks * 128, 128), F32),
            pltpu.VMEM((2 * nodes, 128), BF16),
            pltpu.VMEM((128, width), BF16),
            pltpu.VMEM((2 * nodes, width), BF16),
            pltpu.VMEM((groups, width, 3 * gw), BF16),
            pltpu.VMEM((width, width), BF16),
            pltpu.VMEM((nodes, gw), BF16),
            pltpu.VMEM((2 * nodes, gw), BF16),
            pltpu.VMEM((2 * nodes, gw), BF16),
            pltpu.VMEM((groups, nodes, gw), BF16),
            dma((3 * groups + 1,)),
            dma((2,)), dma((2,)), dma((2,)), dma((2,)),
            dma((groups + 1, n - 1)), dma((groups + 1, n - 1)),
            dma((groups + 1, 2)), dma((groups + 1, 2)),
            dma((groups + 1, n - 1)), dma((groups + 1, n - 1)),
        ],
        compiler_params=pltpu.CompilerParams(
            collective_id=0, has_side_effects=True, vmem_limit_bytes=60 * 2**20),
    )(cell_index, fields[0], interp_weight, w_in, ln_gain[None], w_qkv, w_out)
    return latent[None], update[None]


def solution(mesh):
    placed = (
        P("dp", None, "space"),
        P("space", None),
        P("space", None, None),
        P(),
        P(),
        P("dp", None),
        P("dp", None),
    )
    return jax.shard_map(
        functools.partial(shards, mesh.shape["dp"], mesh.shape["space"]),
        mesh=mesh,
        in_specs=placed,
        out_specs=(P("dp", "space", None), P("dp", "space", None)),
        check_vma=False,
    )
```

time: 191 us -> 76.8 us (0.40)
  waiting for transfers between devices: 81 us -> 0 us
  Pallas kernels: 0 us -> 71.6 us
  local copies, waits for them, and re-layouts: 44 us -> 3.32 us
  matrix products: 25.3 us -> 0 us
  other arithmetic: 15.5 us -> 0 us
  between operations: 14.3 us -> 0.65 us
  loops' own time: 5.78 us -> 0 us
  starting transfers between devices: 4.75 us -> 0 us
    pallas_call x0 -> x1, Pallas kernels: none -> 71.6 us  [shards(): pl.pallas_call(functools.partial(kernel, n, space), out_shape=[jax.ShapeD...]
    all_gather x2 -> x0, waiting for transfers between devices: 46.3 us -> none  [the longest x1 46.3 us: shards(): lax.all_gather(w_qkv, 'dp', axis=0, tiled=True)]
    ppermute x4 -> x0, waiting for transfers between devices: 34 us -> none  [the longest x2 24.6 us: padded(): before = lax.ppermute(last, axis, up)]
    dot_general x20 -> x0, matrix products: 25.3 us -> none  [the longest x8 7.36 us: attend(): jnp.einsum('hqk,khd->qhd', probs, value_group, preferred_element_type=jnp...]
    dynamic_slice x32 -> x0, local copies, waits for them, and re-layouts: 14.5 us -> none  [the longest x8 8.56 us: attend(): lax.dynamic_slice_in_dim(window, offset, group_width, 1)]
    gather x2 -> x0, local copies, waits for them, and re-layouts: 12.8 us -> none  [shards(): picked = jnp.take(extended, cell_index, axis=1)]
    while x1 -> x0, local copies, waits for them, and re-layouts: 6.49 us -> none  [shards(): grouped = lax.map(attend, jnp.arange(HEADS // 2, dtype=jnp.int32))]
    concatenate x3 -> x0, other arithmetic: 5.91 us -> none  [the longest x2 4.4 us: padded(): array = jnp.concatenate([before, array, after], axis=dim)]
  transfers between devices with their start and end apart: 6 -> 0, of which waited for: 5 -> 0; matrix products, arithmetic and copies ran while one was open for 29% -> 0% of each run, Pallas kernels for 0% -> 0%
where the time goes in v1:
time: 76.8 us; the launch traced here: 75.6 us
  Pallas kernels  71.6 us (93%)
  local copies, waits for them, and re-layouts  3.32 us (4%)
    pallas_call x1, Pallas kernels, shards(): pl.pallas_call(functools.partial(kernel, n, space), out_shape=[jax.ShapeD...  71.6 us
    unnamed x4, local copies, waits for them, and re-layouts  3.32 us

profile of v1, /device:TPU:1, one launch (start us, length us, event | category | flops | bytes accessed | tf_op | source)
XLA Modules:
  0.0 75.6 jit_solution(16549569455516519766)
XLA Ops:
  0.6 71.6 %shard_map.86 = (bf16[512,1024]{1,0:T(8,128)(2,1)}, bf16[512,1024]{1,0:T(8,128)(2,1)}) custom-call(s32[32,128]{1,0:T(8,128)} %index_ref.1, bf16[100,4096]{1,0:T(8,128)(2,1)} %bitcast.6, bf16[32,16,128]{2,1,0:T(8,128)(2,1)} %weight_ref.1, bf16[100,1024]{1,0:T(8,128)(2,1)} %w_in_ref.1, f32[1,1024]{1,0:T(1,128)} %bitcast.7, bf16[256,3072]{1,0:T(8,128)(2,1)} %w_qkv_ref.1, ...), custom_call_target="tpu_custom_call" | custom-call | tf_op jit(solution)/shard_map/pallas_call | solution.py:304
  72.3 0.0 copy-start
  72.3 2.4 %copy.11 = bf16[1,512,1024]{2,1,0:T(8,128)(2,1)} copy(bf16[1,512,1024]{2,1,0:T(8,128)(2,1)} %bitcast.5) | data formatting | bytes 2097152
  74.6 0.0 copy-done
  74.6 1.0 %copy.12 = bf16[1,512,1024]{2,1,0:T(8,128)(2,1)} copy(bf16[1,512,1024]{2,1,0:T(8,128)(2,1)S(1)} %bitcast.4) | data formatting | bytes 2097152
Async XLA Ops:
  72.3 2.4 %copy-start = (bf16[512,1024]{1,0:T(8,128)(2,1)S(1)}, bf16[512,1024]{1,0:T(8,128)(2,1)}, u32[]{:S(2)}) copy-start(bf16[512,1024]{1,0:T(8,128)(2,1)} %get-tuple-element.5) | copy-start | bytes 3145732

commit v2 on v1

--- a/solution.py
+++ b/solution.py
@@ -15,10 +15,10 @@
 
 def kernel(
     n, space, index_ref, field_ref, weight_ref, w_in_ref, gain_ref, w_qkv_ref, w_out_ref,
-    latent_ref, update_ref,
+    att_out, w_out_full, enc_out,
     low_ref, high_ref, cells_ref, picked_ref, enc_ref, w_in_full, normed_ref, qkv_ref, out_ref,
     q_ref, k_ref, v_ref, att_ref,
-    local_sem, field_send, field_recv, enc_send, enc_recv,
+    local_sem, leave_sem, field_send, field_recv, enc_send, enc_recv,
     a_send, a_recv, f_send, f_recv, p_send, p_recv,
 ):
     d, s = lax.axis_index("dp"), lax.axis_index("space")
@@ -34,7 +34,7 @@
     groups, _, gw3 = qkv_ref.shape
     gw = gw3 // 3
     head_size = gw // GROUP_HEADS
-    nodes = latent_ref.shape[0]
+    nodes = att_out.shape[0]
     margin = nodes // 2
     window = nodes + 2 * margin
     blocks, per_block, slots = weight_ref.shape
@@ -134,6 +134,7 @@
 
     begin(0)
     begin(1)
+    begin(2)
 
     unit = (lax.broadcasted_iota(jnp.int32, (channels, 128), 0)
             == lax.broadcasted_iota(jnp.int32, (channels, 128), 1)).astype(BF16)
@@ -143,7 +144,7 @@
             source[:, pl.ds(start, 512)], unit, (((0,), (0,)), ((), ())),
             preferred_element_type=F32)
 
-    @pl.loop(0, cell_count // 512)
+    @pl.loop(0, cell_count // 512, unroll=2)
     def _(i):
         turn(field_ref, pl.multiple_of(i * 512, 512), pl.multiple_of(reach + i * 512, 512))
 
@@ -169,7 +170,7 @@
 
     gather(0, blocks // 2)
     forward(0)
-    begin(2)
+    begin(3)
     gather(blocks // 2, blocks)
 
     per_step = 8
@@ -189,33 +190,32 @@
                       enc_send.at[1], enc_recv.at[1], (d, down))
     enc_up.start()
     enc_down.start()
+    enc_leave = pltpu.make_async_copy(enc_ref.at[pl.ds(margin, nodes), :], enc_out, leave_sem.at[0])
+    enc_leave.start()
     forward(1)
-    begin(3)
-
-    def embed(start, own):
+    begin(groups)
+
+    def embed(start):
         embedded = jnp.dot(enc_ref[pl.ds(start, 128), :], w_in_full[...], preferred_element_type=F32)
-        if own:
-            latent_ref[pl.ds(start - margin, 128), :] = embedded.astype(BF16)
         average = jnp.mean(embedded, axis=1, keepdims=True)
         centered = embedded - average
         spread = jnp.mean(centered * centered, axis=1, keepdims=True)
         normed_ref[pl.ds(start, 128), :] = (
             centered * lax.rsqrt(spread + 1e-05) * gain_ref[...]).astype(BF16)
 
-    @pl.loop(0, nodes // 128)
-    def _(i):
-        embed(pl.multiple_of(margin + i * 128, 128), True)
+    @pl.loop(0, nodes // 128, unroll=2)
+    def _(i):
+        embed(pl.multiple_of(margin + i * 128, 128))
 
     enc_up.wait_recv()
     enc_down.wait_recv()
 
     @pl.loop(0, margin // 128)
     def _(i):
-        embed(pl.multiple_of(i * 128, 128), False)
-        embed(pl.multiple_of(margin + nodes + i * 128, 128), False)
+        embed(pl.multiple_of(i * 128, 128))
+        embed(pl.multiple_of(margin + nodes + i * 128, 128))
 
     forward(2)
-    begin(4)
 
     same_head = (lax.broadcasted_iota(jnp.int32, (gw, gw), 0) // head_size
                  == lax.broadcasted_iota(jnp.int32, (gw, gw), 1) // head_size).astype(BF16)
@@ -229,38 +229,44 @@
                  + jnp.dot(rest, same_head, preferred_element_type=F32))
         return (block * lax.rsqrt(total * (1.0 / head_size) + 1e-06)).astype(BF16) * scale
 
+    scale = jnp.asarray(head_size ** -0.5, BF16)
+    one = jnp.asarray(1.0, BF16)
+
     def compute(g):
-        @pl.loop(0, window // 256)
-        def _(i):
-            span = pl.ds(pl.multiple_of(i * 256, 256), 256)
+        for i in range(window // 512):
+            span = pl.ds(i * 512, 512)
             part = jnp.dot(normed_ref[span, :], qkv_ref[g, :, pl.ds(gw, 2 * gw)],
                            preferred_element_type=F32)
-            k_ref[span, :] = unit_heads(part[:, :gw], jnp.asarray(1.0, BF16))
+            k_ref[span, :] = unit_heads(part[:, :gw], one)
             v_ref[span, :] = part[:, gw:].astype(BF16)
-
-        scale = jnp.asarray(head_size ** -0.5, BF16)
-
-        @pl.loop(0, nodes // 256)
-        def _(i):
-            part = jnp.dot(normed_ref[pl.ds(pl.multiple_of(margin + i * 256, 256), 256), :],
-                           qkv_ref[g, :, pl.ds(0, gw)], preferred_element_type=F32)
-            q_ref[pl.ds(pl.multiple_of(i * 256, 256), 256), :] = unit_heads(part, scale)
-
-        @pl.loop(0, nodes // 128)
+        part = jnp.dot(normed_ref[pl.ds(margin, nodes), :], qkv_ref[g, :, pl.ds(0, gw)],
+                       preferred_element_type=F32)
+        q_ref[...] = unit_heads(part, scale)
+
+        @pl.loop(0, nodes // 128, unroll=2)
         def _(i):
             span = pl.ds(pl.multiple_of(i * 128, 128), 128)
             queries = q_ref[span, :]
             head_of = lax.broadcasted_iota(jnp.int32, (128, gw), 1) // head_size
-            mixed = jnp.zeros((128, gw), F32)
-            for h in range(GROUP_HEADS):
-                mine = head_of == h
-                scores = lax.dot_general(jnp.where(mine, queries, jnp.zeros_like(queries)),
-                                         k_ref[...], contract_last, preferred_element_type=F32)
-                weights = jnp.exp(scores)
-                total = jnp.sum(weights, axis=1, keepdims=True)
-                out = jnp.dot(weights.astype(BF16), v_ref[...], preferred_element_type=F32)
-                mixed = jnp.where(mine, out * (1.0 / total), mixed)
+            stacked = jnp.concatenate(
+                [jnp.where(head_of == h, queries, jnp.zeros_like(queries))
+                 for h in range(GROUP_HEADS)], axis=0)
+            scores = lax.dot_general(stacked, k_ref[...], contract_last,
+                                     preferred_element_type=F32)
+            weights = jnp.exp(scores)
+            total = jnp.sum(weights, axis=1, keepdims=True)
+            out = jnp.dot(weights.astype(BF16), v_ref[...], preferred_element_type=F32)
+            out = out * (1.0 / total)
+            mixed = out[:128]
+            for h in range(1, GROUP_HEADS):
+                mixed = jnp.where(head_of == h, out[h * 128:(h + 1) * 128], mixed)
             att_ref[g, span, :] = mixed.astype(BF16)
+
+    def leave(g):
+        return pltpu.make_async_copy(
+            att_ref.at[g], att_out.at[:, pl.ds(g * gw, gw)], leave_sem.at[2 + g])
+
+    w_out_leave = pltpu.make_async_copy(out_ref, w_out_full, leave_sem.at[1])
 
     @pl.loop(0, groups)
     def _(g):
@@ -269,25 +275,31 @@
             def _():
                 finish(c)
                 if c + 3 <= groups:
-                    if c + 3 > 2:
-                        forward(c + 3)
+                    forward(c + 3)
+                if c:
+                    leave(c - 1).start()
+                if c == groups - 1:
+                    finish(groups)
+                    w_out_leave.start()
         compute(g)
 
-    finish(groups)
-
-    @pl.loop(0, nodes // 128)
-    def _(i):
-        span = pl.ds(pl.multiple_of(i * 128, 128), 128)
-        total = jnp.zeros((128, width), F32)
-        for g in range(groups):
-            total += jnp.dot(att_ref[g, span, :], out_ref[pl.ds(g * gw, gw), :],
-                             preferred_element_type=F32)
-        update_ref[span, :] = total.astype(BF16)
-
+    leave(groups - 1).start()
+    for g in range(groups):
+        leave(g).wait()
+    w_out_leave.wait()
+    enc_leave.wait()
     for copy in (field_up, field_down, enc_up, enc_down):
         copy.wait_send()
     for c in range(groups + 1):
         drain(c)
+
+
+def project(enc_ref, w_in_ref, att_ref, w_out_ref, latent_ref, update_ref):
+    channels = w_in_ref.shape[0]
+    latent_ref[...] = jnp.dot(enc_ref[:, :channels], w_in_ref[...],
+                              preferred_element_type=F32).astype(BF16)
+    update_ref[...] = jnp.dot(att_ref[...], w_out_ref[...],
+                              preferred_element_type=F32).astype(BF16)
 
 
 def shards(n, space, fields, cell_index, interp_weight, w_in, ln_gain, w_qkv, w_out):
@@ -301,11 +313,12 @@
     vmem = pl.BlockSpec(memory_space=pltpu.VMEM)
     hbm = pl.BlockSpec(memory_space=pl.ANY)
     dma = pltpu.SemaphoreType.DMA
-    latent, update = pl.pallas_call(
+    attended, w_out_full, encoded = pl.pallas_call(
         functools.partial(kernel, n, space),
-        out_shape=[jax.ShapeDtypeStruct((nodes, width), BF16)] * 2,
+        out_shape=[jax.ShapeDtypeStruct(shape, BF16)
+                   for shape in ((nodes, width), (width, width), (nodes, 128))],
         in_specs=[pl.BlockSpec(memory_space=pltpu.SMEM), vmem, vmem, vmem, vmem, hbm, hbm],
-        out_specs=[vmem, vmem],
+        out_specs=[hbm, hbm, hbm],
         scratch_shapes=[
             pltpu.VMEM((channels, reach), BF16),
             pltpu.VMEM((channels, reach), BF16),
@@ -320,7 +333,7 @@
             pltpu.VMEM((2 * nodes, gw), BF16),
             pltpu.VMEM((2 * nodes, gw), BF16),
             pltpu.VMEM((groups, nodes, gw), BF16),
-            dma((3 * groups + 1,)),
+            dma((3 * groups + 1,)), dma((groups + 2,)),
             dma((2,)), dma((2,)), dma((2,)), dma((2,)),
             dma((groups + 1, n - 1)), dma((groups + 1, n - 1)),
             dma((groups + 1, 2)), dma((groups + 1, 2)),
@@ -329,6 +342,21 @@
         compiler_params=pltpu.CompilerParams(
             collective_id=0, has_side_effects=True, vmem_limit_bytes=60 * 2**20),
     )(cell_index, fields[0], interp_weight, w_in, ln_gain[None], w_qkv, w_out)
+    step = nodes // 2
+
+    def by_row(size):
+        return pl.BlockSpec((step, size), lambda i: (i, 0))
+
+    def whole(array):
+        return pl.BlockSpec(array.shape, lambda i: (0, 0))
+
+    latent, update = pl.pallas_call(
+        project,
+        grid=(nodes // step,),
+        out_shape=[jax.ShapeDtypeStruct((nodes, width), BF16)] * 2,
+        in_specs=[by_row(128), whole(w_in), by_row(width), whole(w_out_full)],
+        out_specs=[by_row(width), by_row(width)],
+    )(encoded, w_in, attended, w_out_full)
     return latent[None], update[None]
 
 

time: 76.8 us -> 61.3 us (0.80); the launches traced: 75.6 us -> 61.1 us
  Pallas kernels: 71.6 us -> 60.5 us
  local copies, waits for them, and re-layouts: 3.32 us -> 0 us
    pallas_call x1, Pallas kernels: 71.6 us -> 56.1 us  [shards(): pl.pallas_call(functools.partial(kernel, n, space), out_shape=[jax.ShapeD...]
    pallas_call x0 -> x1, Pallas kernels: none -> 4.36 us  [shards(): pl.pallas_call(project, grid=(nodes // step,), out_shape=[jax.ShapeDtypeS...]
    unnamed x4 -> x0, local copies, waits for them, and re-layouts: 3.32 us -> none
where the time goes in v2:
time: 61.3 us; the launch traced here: 61.1 us
  Pallas kernels  60.5 us (99%)
  between operations  0.64 us (1%)
    pallas_call x1, Pallas kernels, shards(): pl.pallas_call(functools.partial(kernel, n, space), out_shape=[jax.ShapeD...  56.1 us
    pallas_call x1, Pallas kernels, shards(): pl.pallas_call(project, grid=(nodes // step,), out_shape=[jax.ShapeDtypeS...  4.36 us

profile of v2, /device:TPU:1, one launch (start us, length us, event | category | flops | bytes accessed | tf_op | source)
XLA Modules:
  0.0 61.1 jit_solution(15800933058970132697)
XLA Ops:
  0.6 56.1 %shard_map.86 = (bf16[512,1024]{1,0:T(8,128)(2,1)}, bf16[1024,1024]{1,0:T(8,128)(2,1)}, bf16[512,128]{1,0:T(8,128)(2,1)}) custom-call(s32[32,128]{1,0:T(8,128)} %index_ref.1, bf16[100,4096]{1,0:T(8,128)(2,1)} %bitcast.4, bf16[32,16,128]{2,1,0:T(8,128)(2,1)} %weight_ref.1, bf16[100,1024]{1,0:T(8,128)(2,1)} %w_in_ref.3, f32[1,1024]{1,0:T(1,128)} %bitcast.5, ...), custom_call_target="tpu_custom_call" | custom-call | tf_op jit(solution)/shard_map/pallas_call | solution.py:316
  56.7 4.4 %shard_map.87 = (bf16[512,1024]{1,0:T(8,128)(2,1)}, bf16[512,1024]{1,0:T(8,128)(2,1)}) custom-call(bf16[512,128]{1,0:T(8,128)(2,1)} %get-tuple-element.7.enc_ref, bf16[100,1024]{1,0:T(8,128)(2,1)} %w_in_ref.3, bf16[512,1024]{1,0:T(8,128)(2,1)} %get-tuple-element.8.att_ref, bf16[1024,1024]{1,0:T(8,128)(2,1)} %get-tuple-element.9.w_out_ref), custom_call_target="tpu_custom_call" | custom-call | tf_op jit(solution)/shard_map/pallas_call | solution.py:353
